TPU v7x, 32 devices: a whole 2x2x4 slice. The times are simulated.
32 devices in a mesh: dp: 8 (over z, y), tensor: 4 (over x, core).
Axes of the slice: x: 2, y: 2, z: 4, core: 2. Of those that a mesh axis runs over, the one named last changes fastest.
Arguments:
- patches: bfloat16 [8192, 1280], P('dp', 'tensor'), may hold values from -60 to 60
- counts: int32 [16], replicated, may hold values from 0 to 512, as said below
- first_gain: float32 [1280], replicated, may hold values from 0.1 to 1.9
- first_shift: float32 [1280], replicated, may hold values from -3 to 3
- in_weight: bfloat16 [1280, 3, 1280], P(None, None, 'tensor'), may hold values from -0.15625 to 0.15625
- in_bias: float32 [3, 1280], P(None, 'tensor'), may hold values from -30 to 30
- out_weight: bfloat16 [1280, 1280], P(None, 'tensor'), may hold values from -0.15625 to 0.15625
- out_bias: float32 [1280], P('tensor'), may hold values from -3 to 3
- second_gain: float32 [1280], P('tensor'), may hold values from 0.1 to 1.9
- second_shift: float32 [1280], P('tensor'), may hold values from -3 to 3
- merger_weight: bfloat16 [4, 1280, 4096], P(None, 'tensor', 'dp'), may hold values from -0.078125 to 0.078125
- merger_bias: float32 [4096], replicated, may hold values from -4 to 4
Outputs:
- embeds: bfloat16 [2048, 4096], P(('dp', 'tensor'))
Inputs may be any that keep to these rules, and one draw needn't show every extreme that they name: Entry 2 r + j is the patch count of slot j of data rank r, 0 for an empty slot; a rank's images fill its slots from slot 0; counts are multiples of 4; ranks 2 i and 2 i + 1 hold at most two images together, and in every draw some rank holds two.
All inputs are finite; a program needn't handle non-finite values.
Results may differ from a plain program's by a relative error of at most 0.0095.
Values may be sent and summed in bfloat16 or wider, within the bound.
No kernel may reach another device: no remote copies, remote signals or barrier semaphores. Data moves between devices by JAX's collectives and lax.ppermute only.
A program may use at most 128 MiB of HBM per device.

v0:
```python
import math
import jax
import jax.numpy as jnp
from jax import lax
from jax.sharding import PartitionSpec as P

D = 1280
HEADS = 16
LLMW = 4096
TILE = 512
SLOTS = 2
EPS = 1e-06
MASKED = -1e30


def from_partner(x, axis, stride):
    return lax.ppermute(x, axis, [(i, i ^ 1 << stride) for i in range(lax.axis_size(axis))])


def layer_norm(values, gain, shift):
    row_mean = jnp.mean(values, axis=-1, keepdims=True)
    centred = values - row_mean
    spread = jnp.mean(centred * centred, axis=-1, keepdims=True)
    return centred * lax.rsqrt(spread + EPS) * gain + shift


def encode(
    shard,
    slot_counts,
    first_gain,
    first_shift,
    in_weight,
    in_bias,
    out_weight,
    out_bias,
    second_gain,
    second_shift,
):
    number = slot_counts.shape[0]
    local_width = shard.shape[1]
    head_size = D // HEADS
    local_heads = local_width // head_size
    scale = 1.0 / math.sqrt(head_size)
    whole = lax.all_gather(shard, "tensor", axis=1, tiled=True)
    values = whole.astype(jnp.float32)
    normed = layer_norm(values, first_gain, first_shift).astype(jnp.bfloat16)
    projected = jnp.dot(
        normed, in_weight.reshape(D, 3 * local_width), preferred_element_type=jnp.float32
    )
    projected = (projected + in_bias.reshape(3 * local_width)).astype(jnp.bfloat16)
    projected = projected.reshape(number, TILE, 3, local_heads, head_size)
    queries = projected[:, :, 0]
    keys_tile = projected[:, :, 1]
    values_tile = projected[:, :, 2]
    scores = (
        jnp.einsum("nqhd,nkhd->nhqk", queries, keys_tile, preferred_element_type=jnp.float32)
        * scale
    )
    positions = jnp.arange(TILE, dtype=jnp.int32)
    key_live = positions[None, :] < slot_counts[:, None]
    scores = jnp.where(key_live[:, None, None, :], scores, MASKED)
    highest = jnp.max(scores, axis=-1, keepdims=True)
    raised = jnp.exp(scores - highest)
    weights = (raised / jnp.sum(raised, axis=-1, keepdims=True)).astype(jnp.bfloat16)
    heads_out = jnp.einsum(
        "nhqk,nkhd->nqhd", weights, values_tile, preferred_element_type=jnp.float32
    )
    heads_out = heads_out.astype(jnp.bfloat16).reshape(number * TILE, local_width)
    all_heads = lax.all_gather(heads_out, "tensor", axis=1, tiled=True)
    residual = (
        shard.astype(jnp.float32)
        + jnp.dot(all_heads, out_weight, preferred_element_type=jnp.float32)
        + out_bias
    )
    row_sum, row_squares = lax.psum(
        (jnp.sum(residual, axis=1), jnp.sum(residual * residual, axis=1)), "tensor"
    )
    row_mean = (row_sum / D)[:, None]
    second = (row_squares / D)[:, None]
    encoded = (residual - row_mean) * lax.rsqrt(
        second - row_mean * row_mean + EPS
    ) * second_gain + second_shift
    return encoded.astype(jnp.bfloat16).reshape(number * TILE // 4, 4 * local_width)


def rank_bit(rank, bit):
    return jnp.bitwise_and(jnp.right_shift(rank, bit), 1) == 1


def per_device(
    patches,
    counts,
    first_gain,
    first_shift,
    in_weight,
    in_bias,
    out_weight,
    out_bias,
    second_gain,
    second_shift,
    merger_weight,
    merger_bias,
):
    rank = lax.axis_index("dp")
    mine = lax.dynamic_slice_in_dim(counts, rank * SLOTS, SLOTS)
    weights_args = (
        first_gain,
        first_shift,
        in_weight,
        in_bias,
        out_weight,
        out_bias,
        second_gain,
        second_shift,
    )
    merged = encode(patches, mine, *weights_args)
    groups = lax.axis_size("tensor")
    quarter = SLOTS * TILE // 4 // groups
    ranks = lax.axis_size("dp")
    levels = ranks.bit_length() - 1
    rows_held = merged
    for bit in range(2):
        other = from_partner(rows_held, "dp", bit)
        rows_held = jnp.where(
            rank_bit(rank, bit),
            jnp.concatenate([other, rows_held], axis=0),
            jnp.concatenate([rows_held, other], axis=0),
        )
    column_held = merger_weight
    for bit in range(2, levels):
        other = from_partner(column_held, "dp", bit)
        column_held = jnp.where(
            rank_bit(rank, bit),
            jnp.concatenate([other, column_held], axis=2),
            jnp.concatenate([column_held, other], axis=2),
        )
    block_width = merger_weight.shape[2]
    column_total = column_held.shape[2]
    product = jnp.dot(
        rows_held, column_held.reshape(-1, column_total), preferred_element_type=jnp.float32
    )
    product = product.reshape(4, groups, quarter, column_total)
    summed = lax.psum_scatter(
        product.astype(jnp.bfloat16), "tensor", scatter_dimension=1, tiled=True
    ).astype(jnp.float32)
    within_quartet = jnp.bitwise_and(rank, 3)
    bias_columns = lax.dynamic_index_in_dim(
        merger_bias.reshape(ranks // 4, 4, block_width), within_quartet, 1, keepdims=False
    ).reshape(column_total)
    parcel = (summed + bias_columns).astype(jnp.bfloat16).reshape(2, 2, 1, quarter, column_total)
    for bit in range(2):
        owner_axis = 1 - bit
        high = rank_bit(rank, bit)
        lower_half = lax.index_in_dim(parcel, 0, owner_axis, keepdims=True)
        upper_half = lax.index_in_dim(parcel, 1, owner_axis, keepdims=True)
        kept = jnp.where(high, upper_half, lower_half)
        sent = jnp.where(high, lower_half, upper_half)
        other = from_partner(sent, "dp", bit)
        parcel = jnp.where(
            high, jnp.concatenate([other, kept], axis=2), jnp.concatenate([kept, other], axis=2)
        )
    parcel = parcel.reshape(4, quarter, ranks // 4, block_width)
    mixed = jnp.transpose(parcel, (1, 2, 0, 3)).reshape(quarter, LLMW)
    row_index = lax.axis_index("tensor") * quarter + jnp.arange(quarter, dtype=jnp.int32)
    slot_of_row = row_index // (TILE // 4)
    within = row_index % (TILE // 4)
    row_count = jnp.sum(
        jnp.where(
            slot_of_row[:, None] == jnp.arange(SLOTS, dtype=jnp.int32)[None, :], mine[None, :], 0
        ),
        axis=1,
    )
    keep = (within * 4 < row_count)[:, None]
    return jnp.where(keep, mixed, jnp.zeros_like(mixed))


def solution(mesh):
    return jax.shard_map(
        per_device,
        mesh=mesh,
        in_specs=(
            P("dp", "tensor"),
            P(),
            P(),
            P(),
            P(None, None, "tensor"),
            P(None, "tensor"),
            P(None, "tensor"),
            P("tensor"),
            P("tensor"),
            P("tensor"),
            P(None, "tensor", "dp"),
            P(),
        ),
        out_specs=P(("dp", "tensor"), None),
        check_vma=False,
    )
```

profile of v0, /device:TPU:0, one launch (start us, length us, event | category | flops | bytes accessed | tf_op | source)
XLA Modules:
  0.0 272.9 jit_solution(12721370287191470557)
XLA Ops:
  6.5 0.0 copy-start
  6.5 0.0 all-gather.3.cloned.1.call-start
  6.5 0.7 all-gather.3.cloned.1.call-update
  7.3 0.0 all-gather.5.cloned.1.call-start
  7.3 0.8 add.107
  8.1 0.7 dynamic_slice.7
  8.8 0.1 iota_compare_fusion
  8.9 28.3 %all-gather.3.cloned.1.call-done = bf16[1024,1280]{0,1:T(8,128)(2,1)} async-done(((bf16[1024,320]{0,1:T(8,128)(2,1)}), bf16[1024,1280]{0,1:T(8,128)(2,1)}) %all-gather.3.cloned.1.call-update) | async-done | bytes 2621456 | tf_op jit(solution)/shard_map/all_gather | solution.py:44
  37.2 2.3 convert_reduce_fusion
  39.5 0.2 copy-done.1
  39.7 0.7 fusion.4
  40.5 0.0 copy-done
  40.5 0.0 copy-done.6
  40.5 4.1 %add_convert_fusion = bf16[1024,960]{0,1:T(8,128)(2,1)} fusion(f32[960]{0:T(1024)S(1)} %add.107, bf16[1280,960]{0,1:T(8,128)(2,1)S(1)} %bitcast.68, bf16[1024,1280]{0,1:T(8,128)(2,1)S(1)} %copy-done.1, f32[1280]{0:T(1024)S(1)} %copy-done.6, f32[1280]{0:T(1024)S(1)} %copy-done.7, f32[1024]{0:T(1024)S(1)} %add_rsqrt_fusion.1, ...), kind=kOutput, calls=%fused_computation.17 | convolution fusion | flops 2526412800 | bytes 7067392 | tf_op jit(solution)/shard_map/dot_general | solution.py:47
  44.6 5.8 %reshape.191 = bf16[2,512,3,4,80]{1,0,4,3,2:T(2,128)(2,1)} reshape(bf16[1024,960]{0,1:T(8,128)(2,1)} %add_convert_fusion) | data formatting | bytes 3932160 | tf_op jit(solution)/shard_map/reshape | solution.py:51
  50.4 3.4 %fusion.46 = (bf16[2,512,1,4,80]{1,0,4,3,2:T(2,128)(2,1)S(1)}, bf16[2,512,1,4,80]{1,0,4,3,2:T(2,128)(2,1)}, bf16[2,512,1,4,80]{1,0,4,3,2:T(2,128)(2,1)}) fusion(bf16[2,512,3,4,80]{1,0,4,3,2:T(2,128)(2,1)} %reshape.191), kind=kLoop, calls=%fused_computation.75 | loop fusion | bytes 3932160 | tf_op jit(solution)/shard_map/slice | solution.py:54
  53.8 7.9 %fusion.47 = (f32[2,4,512]{2,1,0:T(4,128)S(1)}, f32[2,4,512,512]{2,3,1,0:T(8,128)}) fusion(pred[2,512]{1,0:T(4,128)(4,1)S(1)} %iota_compare_fusion, bf16[2,512,1,4,80]{1,0,4,3,2:T(2,128)(2,1)} %get-tuple-element.10, bf16[2,512,1,4,80]{1,0,4,3,2:T(2,128)(2,1)} %get-tuple-element.11), kind=kOutput, calls=%fused_computation.76 | convolution fusion | flops 343933440 | bytes 9716736 | tf_op jit(solution)/shard_map/sub | solution.py:63
  61.7 4.2 %fusion.34 = bf16[2,512,4,80]{1,3,2,0:T(8,128)(2,1)S(1)} fusion(f32[2,4,512,512]{2,3,1,0:T(8,128)} %get-tuple-element.19, f32[2,4,512]{2,1,0:T(4,128)S(1)} %get-tuple-element.18, bf16[2,512,1,4,80]{1,0,4,3,2:T(2,128)(2,1)S(1)} %get-tuple-element.9), kind=kOutput, calls=%fused_computation.40 | convolution fusion | flops 340066304 | bytes 9715712 | tf_op jit(solution)/shard_map/nhqk,nkhd->nqhd/dot_general | solution.py:65
  65.9 0.0 copy-start.2
  65.9 0.0 copy-start.8
  65.9 0.7 copy.45
  66.6 1.0 copy.58
  67.6 0.0 all-gather.5.cloned.1.call-update
  67.6 0.0 copy-start.4
  67.6 0.0 copy-start.5
  67.6 0.2 all-reduce.4.cloned.1.call-start
  67.8 25.4 %all-gather.5.cloned.1.call-done = bf16[1024,1280]{0,1:T(8,128)(2,1)} async-done(((bf16[1024,320]{0,1:T(8,128)(2,1)}), bf16[1024,1280]{0,1:T(8,128)(2,1)}) %all-gather.5.cloned.1.call-update) | async-done | bytes 2621456 | tf_op jit(solution)/shard_map/all_gather | solution.py:69
  93.3 0.0 copy-done.8
  93.3 4.1 %fusion.45 = (f32[1024]{0:T(1024)S(1)}, f32[1024]{0:T(1024)S(1)}, f32[1024,320]{0,1:T(8,128)}) fusion(f32[320]{0:T(512)S(1)} %copy-done.8, bf16[1280,320]{0,1:T(8,128)(2,1)} %param.18, bf16[1024,1280]{0,1:T(8,128)(2,1)} %all-gather.5.cloned.1.call-done, bf16[1024,320]{0,1:T(8,128)(2,1)S(1)} %copy-done.2), kind=kOutput, calls=%fused_computation.74 | convolution fusion | flops 840824832 | bytes 5416192 | tf_op jit(solution)/shard_map/dot_general | solution.py:72
  97.4 6.0 %all-reduce.1 = (f32[1024]{0:T(1024)S(1)}, f32[1024]{0:T(1024)S(1)}) all-reduce(f32[1024]{0:T(1024)S(1)} %get-tuple-element.6, f32[1024]{0:T(1024)S(1)} %get-tuple-element.5), channel_id=1, replica_groups=mesh['dp'=8,'tensor'=4] {'tensor'}, use_global_device_ids=true, to_apply=%region_8.9 | all-reduce | flops 2048 | bytes 16384 | tf_op jit(solution)/shard_map/psum | solution.py:75
  103.4 0.0 copy-done.4
  103.4 0.0 copy-done.5
  103.4 2.4 add_convert_fusion.1
  105.8 1.4 copy.46
  107.3 1.6 reshape.193
  108.8 1.6 collective-permute-start
  110.5 14.8 %collective-permute-done = bf16[256,1280]{1,0:T(8,128)(2,1)S(1)} collective-permute-done((bf16[256,1280]{1,0:T(8,128)(2,1)}, bf16[256,1280]{1,0:T(8,128)(2,1)S(1)}, u32[]{:S(2)}, u32[]{:S(2)}) %collective-permute-start) | collective-permute-done | bytes 655392 | tf_op jit(solution)/shard_map/ppermute | solution.py:17
  125.3 2.7 maximum_select_fusion.2
  128.0 1.5 collective-permute-start.1
  129.5 2.4 collective-permute-start.2
  131.9 53.7 %collective-permute-done.1 = bf16[512,1280]{1,0:T(8,128)(2,1)} collective-permute-done((bf16[512,1280]{1,0:T(8,128)(2,1)}, bf16[512,1280]{1,0:T(8,128)(2,1)}, u32[]{:S(2)}, u32[]{:S(2)}) %collective-permute-start.1) | collective-permute-done | bytes 1310752 | tf_op jit(solution)/shard_map/ppermute | solution.py:17
  185.6 2.8 %maximum_select_fusion = bf16[1024,1280]{1,0:T(8,128)(2,1)S(1)} fusion(bf16[512,1280]{1,0:T(8,128)(2,1)} %maximum_select_fusion.2, bf16[512,1280]{1,0:T(8,128)(2,1)} %collective-permute-done.1, pred[]{:T(512)S(6)} %eq.29), kind=kLoop, calls=%fused_computation.19 | loop fusion | flops 11796480 | bytes 5242881 | tf_op jit(solution)/shard_map/jit(_where)/select_n | solution.py:124
  188.4 0.0 collective-permute-done.2
  188.4 0.0 copy-start.3
  188.5 0.0 copy-start.9
  188.5 7.0 %fusion.27 = bf16[4,4,64,1024]{3,2,1,0:T(8,128)(2,1)} fusion(bf16[4,4,64,1280]{3,2,1,0:T(8,128)(2,1)S(1)} %bitcast.71, bf16[1280,512]{1,0:T(8,128)(2,1)} %bitcast.7, bf16[1280,512]{1,0:T(8,128)(2,1)} %bitcast.6, pred[]{:T(512)S(6)} %eq.31), kind=kOutput, calls=%fused_computation.33 | convolution fusion | flops 2697199616 | bytes 7340033 | tf_op jit(solution)/shard_map/dot_general | solution.py:139
  195.5 0.0 all-reduce.4.cloned.1.call-update
  195.5 0.6 dynamic-slice
  196.1 49.8 %all-reduce.4.cloned.1.call-done = bf16[4,4,64,1024]{3,2,1,0:T(8,128)(2,1)} async-done(((bf16[4,4,64,1024]{3,2,1,0:T(8,128)(2,1)}), bf16[4,4,64,1024]{3,2,1,0:T(8,128)(2,1)}) %all-reduce.4.cloned.1.call-update) | async-done | bytes 2097168
  245.9 1.8 add_convert_fusion.2
  247.8 1.5 collective-permute-start.3
  249.3 6.3 %collective-permute-done.3 = bf16[2,1,1,64,1024]{4,3,1,0,2:T(8,128)(2,1)S(1)} collective-permute-done((bf16[2,1,1,64,1024]{4,3,1,0,2:T(8,128)(2,1)S(1)}, bf16[2,1,1,64,1024]{4,3,1,0,2:T(8,128)(2,1)S(1)}, u32[]{:S(2)}, u32[]{:S(2)}) %collective-permute-start.3) | collective-permute-done | bytes 262176 | tf_op jit(solution)/shard_map/ppermute | solution.py:17
  255.6 0.1 maximum_select_fusion.3
  255.7 0.7 broadcast_select_fusion.4
  256.5 1.5 collective-permute-start.4
  257.9 0.1 fusion.39
  258.0 0.2 concatenate.73
  258.2 0.3 copy.48
  258.5 5.1 %collective-permute-done.4 = bf16[1,1,2,64,1024]{4,3,1,0,2:T(8,128)(2,1)S(1)} collective-permute-done((bf16[1,1,2,64,1024]{4,3,1,0,2:T(8,128)(2,1)}, bf16[1,1,2,64,1024]{4,3,1,0,2:T(8,128)(2,1)S(1)}, u32[]{:S(2)}, u32[]{:S(2)}) %collective-permute-start.4) | collective-permute-done | bytes 262176 | tf_op jit(solution)/shard_map/ppermute | solution.py:17
  263.6 0.2 concatenate.72
  263.8 0.3 copy.47
  264.1 1.0 fusion.38
  265.0 0.4 reshape.196
  265.4 0.9 broadcast_select_fusion
  (15 shorter events, 0.1 us)
Async XLA Ops:
  6.5 33.9 %copy-start = (bf16[1280,3,320]{0,2,1:T(8,128)(2,1)S(1)}, bf16[1280,3,320]{0,2,1:T(8,128)(2,1)}, u32[]{:S(2)}) copy-start(bf16[1280,3,320]{0,2,1:T(8,128)(2,1)} %param.16) | copy-start | bytes 7372804
  6.5 30.6 %all-gather.3.cloned.1.call-start = ((), (), s32[]{:S(2)}) async-start(), calls=%async_computation | async-start | bytes 3276800 | tf_op jit(solution)/shard_map/all_gather | solution.py:44
  7.3 86.0 %all-gather.5.cloned.1.call-start = ((), (), s32[]{:S(2)}) async-start(), calls=%async_computation.1 | async-start | bytes 3276800 | tf_op jit(solution)/shard_map/all_gather | solution.py:69
  8.9 31.6 %copy-start.6 = (f32[1280]{0:T(1024)S(1)}, f32[1280]{0:T(1024)}, u32[]{:S(2)}) copy-start(f32[1280]{0:T(1024)} %param.15) | copy-start | bytes 15364
  37.2 2.5 copy-start.1
  37.2 3.3 %copy-start.7 = (f32[1280]{0:T(1024)S(1)}, f32[1280]{0:T(1024)}, u32[]{:S(2)}) copy-start(f32[1280]{0:T(1024)} %param.14) | copy-start | bytes 15364
  65.9 27.4 %copy-start.2 = (bf16[1024,320]{0,1:T(8,128)(2,1)S(1)}, bf16[1024,320]{0,1:T(8,128)(2,1)}, u32[]{:S(2)}) copy-start(bf16[1024,320]{0,1:T(8,128)(2,1)} %param.12) | copy-start | bytes 1966084
  65.9 27.4 %copy-start.8 = (f32[320]{0:T(512)S(1)}, f32[320]{0:T(512)}, u32[]{:S(2)}) copy-start(f32[320]{0:T(512)} %param.19) | copy-start | bytes 3844
  67.6 35.8 %copy-start.4 = (f32[320]{0:T(512)S(1)}, f32[320]{0:T(512)}, u32[]{:S(2)}) copy-start(f32[320]{0:T(512)} %param.21) | copy-start | bytes 3844
  67.6 35.8 %copy-start.5 = (f32[320]{0:T(512)S(1)}, f32[320]{0:T(512)}, u32[]{:S(2)}) copy-start(f32[320]{0:T(512)} %param.20) | copy-start | bytes 3844
  67.6 178.3 %all-reduce.4.cloned.1.call-start = ((), (), s32[]{:S(2)}) async-start(), calls=%async_computation.2 | async-start | bytes 4194304
  108.8 16.4 %collective-permute-start = (bf16[256,1280]{1,0:T(8,128)(2,1)}, bf16[256,1280]{1,0:T(8,128)(2,1)S(1)}, u32[]{:S(2)}, u32[]{:S(2)}) collective-permute-start(bf16[256,1280]{1,0:T(8,128)(2,1)} %reshape.193), channel_id=1, source_target_pairs={{0,4},{4,0},{8,12},{12,8},{16,20},{20,16},{24,28},{28,24},{1,5},{5... | collective-permute-start | bytes 1966088 | tf_op jit(solution)/shard_map/ppermute | solution.py:17
  128.0 57.6 %collective-permute-start.1 = (bf16[512,1280]{1,0:T(8,128)(2,1)}, bf16[512,1280]{1,0:T(8,128)(2,1)}, u32[]{:S(2)}, u32[]{:S(2)}) collective-permute-start(bf16[512,1280]{1,0:T(8,128)(2,1)} %maximum_select_fusion.2), channel_id=1, source_target_pairs={{0,8},{4,12},{8,0},{12,4},{16,24},{20,28},{24,16},{28,20},{1,9},{5... | collective-permute-start | bytes 3932168 | tf_op jit(solution)/shard_map/ppermute | solution.py:17
  129.5 58.9 %collective-permute-start.2 = (bf16[4,320,512]{2,1,0:T(8,128)(2,1)}, bf16[4,320,512]{2,1,0:T(8,128)(2,1)}, u32[]{:S(2)}, u32[]{:S(2)}) collective-permute-start(bf16[4,320,512]{2,1,0:T(8,128)(2,1)} %param.22), channel_id=1, source_target_pairs={{0,16},{4,20},{8,24},{12,28},{16,0},{20,4},{24,8},{28,12},{1,17},{... | collective-permute-start | bytes 3932168 | tf_op jit(solution)/shard_map/ppermute | solution.py:17
  188.4 7.0 %copy-start.3 = (f32[4096]{0:T(1024)S(1)}, f32[4096]{0:T(1024)}, u32[]{:S(2)}) copy-start(f32[4096]{0:T(1024)} %param.23) | copy-start | bytes 49156
  188.5 7.1 %copy-start.9 = (u32[32]{0:T(128)S(1)}, u32[32]{0:T(128)}, u32[]{:S(2)}) copy-start(u32[32]{0:T(128)} %constant.74) | copy-start | bytes 388
  247.8 7.9 %collective-permute-start.3 = (bf16[2,1,1,64,1024]{4,3,1,0,2:T(8,128)(2,1)S(1)}, bf16[2,1,1,64,1024]{4,3,1,0,2:T(8,128)(2,1)S(1)}, u32[]{:S(2)}, u32[]{:S(2)}) collective-permute-start(bf16[2,1,1,64,1024]{4,3,1,0,2:T(8,128)(2,1)S(1)} %get-tuple-element.14), channel_id=1, source_target_pairs={{0,4},{4,0},{8,12},{12,8},{16,20},{20,16},{24,28},{28,24},{1,5},{5... | collective-permute-start | bytes 786440 | tf_op jit(solution)/shard_map/ppermute | solution.py:17
  256.5 7.2 %collective-permute-start.4 = (bf16[1,1,2,64,1024]{4,3,1,0,2:T(8,128)(2,1)}, bf16[1,1,2,64,1024]{4,3,1,0,2:T(8,128)(2,1)S(1)}, u32[]{:S(2)}, u32[]{:S(2)}) collective-permute-start(bf16[1,1,2,64,1024]{4,3,1,0,2:T(8,128)(2,1)} %get-tuple-element.12), channel_id=1, source_target_pairs={{0,8},{4,12},{8,0},{12,4},{16,24},{20,28},{24,16},{28,20},{1,9},{5... | collective-permute-start | bytes 786440 | tf_op jit(solution)/shard_map/ppermute | solution.py:17
Sparse Core Ops, SparseCore 0:
  8.9 28.2 all-gather.2
  67.7 25.5 all-gather.4
  195.6 50.2 all-reduce.3
where the time goes:
time: 273 us
  waiting for transfers between devices  184 us (67%)
  matrix products  27.4 us (10%)
  local copies, waits for them, and re-layouts  17.4 us (6%)
  other arithmetic  15.7 us (6%)
  between operations  13.4 us (5%)
  starting transfers between devices  8.81 us (3%)
  blocking collectives  5.97 us (2%)
    ppermute x5, waiting for transfers between devices, from_partner(): lax.ppermute(x, axis, [(i, i ^ 1 << stride) for i in range(lax.axis_size(...  80 us
    unnamed x4, waiting for transfers between devices  50.5 us
    all_gather x1, waiting for transfers between devices, encode(): whole = lax.all_gather(shard, 'tensor', axis=1, tiled=True)  28.3 us
    all_gather x1, waiting for transfers between devices, encode(): all_heads = lax.all_gather(heads_out, 'tensor', axis=1, tiled=True)  25.4 us
    ppermute x5, starting transfers between devices, from_partner(): lax.ppermute(x, axis, [(i, i ^ 1 << stride) for i in range(lax.axis_size(...  8.55 us
    sub x1, matrix products, encode(): raised = jnp.exp(scores - highest)  7.88 us
    dot_general x1, matrix products, per_device(): jnp.dot(rows_held, column_held.reshape(-1, column_total), preferred_eleme...  6.99 us
    psum x1, blocking collectives, encode(): lax.psum((jnp.sum(residual, axis=1), jnp.sum(residual * residual, axis=1)...  5.97 us
  transfers between devices with their start and end apart: 8, of which 7 were waited for; matrix products, arithmetic and copies ran while one was open for 2% of the time, Pallas kernels for 0%

commit v1 on v0

--- a/solution.py
+++ b/solution.py
@@ -41,7 +41,14 @@
     head_size = D // HEADS
     local_heads = local_width // head_size
     scale = 1.0 / math.sqrt(head_size)
-    whole = lax.all_gather(shard, "tensor", axis=1, tiled=True)
+    ring = [shard]
+    for hop in range(3):
+        ring.append(lax.ppermute(ring[-1], "tensor", [(dev, (dev + 1) % 4) for dev in range(4)]))
+    whole = jnp.roll(
+        jnp.concatenate(ring[::-1], axis=1),
+        (lax.axis_index("tensor") + 1) * ring[0].shape[1],
+        axis=1,
+    )
     values = whole.astype(jnp.float32)
     normed = layer_norm(values, first_gain, first_shift).astype(jnp.bfloat16)
     projected = jnp.dot(

time: 273 us -> 281 us (1.029)
  local copies, waits for them, and re-layouts: 17.4 us -> 22.8 us
  waiting for transfers between devices: 184 us -> 187 us
    ppermute x0 -> x3, waiting for transfers between devices: none -> 29.2 us  [encode(): lax.ppermute(ring[-1], 'tensor', [(dev, (dev + 1) % 4) for dev in range(4)])]
    all_gather x1 -> x0, waiting for transfers between devices: 28.3 us -> none  [encode(): whole = lax.all_gather(shard, 'tensor', axis=1, tiled=True)]
    unnamed x22 -> x31, local copies, waits for them, and re-layouts: 1.76 us -> 7.08 us
    unnamed x4 -> x3, waiting for transfers between devices: 50.5 us -> 49.8 us
  transfers between devices with their start and end apart: 8 -> 10, of which waited for: 7 -> 9; matrix products, arithmetic and copies ran while one was open for 2% -> 2% of each run, Pallas kernels for 0% -> 0%
where the time goes in v1:
time: 281 us; the launch traced here: 280 us
  waiting for transfers between devices  187 us (67%)
  matrix products  27.6 us (10%)
  local copies, waits for them, and re-layouts  22.8 us (8%)
  other arithmetic  14.5 us (5%)
  between operations  13.7 us (5%)
  starting transfers between devices  9.1 us (3%)
  blocking collectives  5.97 us (2%)
    ppermute x5, waiting for transfers between devices, from_partner(): lax.ppermute(x, axis, [(i, i ^ 1 << stride) for i in range(lax.axis_size(...  80 us
    unnamed x3, waiting for transfers between devices  49.8 us
    ppermute x3, waiting for transfers between devices, encode(): lax.ppermute(ring[-1], 'tensor', [(dev, (dev + 1) % 4) for dev in range(4)])  29.2 us
    all_gather x1, waiting for transfers between devices, encode(): all_heads = lax.all_gather(heads_out, 'tensor', axis=1, tiled=True)  27.6 us
    ppermute x5, starting transfers between devices, from_partner(): lax.ppermute(x, axis, [(i, i ^ 1 << stride) for i in range(lax.axis_size(...  8.55 us
    sub x1, matrix products, encode(): raised = jnp.exp(scores - highest)  7.9 us
    unnamed x31, local copies, waits for them, and re-layouts  7.08 us
    dot_general x1, matrix products, per_device(): jnp.dot(rows_held, column_held.reshape(-1, column_total), preferred_eleme...  6.96 us
  transfers between devices with their start and end apart: 10, of which 9 were waited for; matrix products, arithmetic and copies ran while one was open for 2% of the time, Pallas kernels for 0%

profile of v1, /device:TPU:0, one launch (start us, length us, event | category | flops | bytes accessed | tf_op | source)
XLA Modules:
  0.0 280.4 jit_solution(15891813722138344927)
XLA Ops:
  6.5 0.5 collective-permute-start
  7.0 10.4 %collective-permute-done = bf16[1024,320]{0,1:T(8,128)(2,1)S(1)} collective-permute-done((bf16[1024,320]{0,1:T(8,128)(2,1)}, bf16[1024,320]{0,1:T(8,128)(2,1)S(1)}, u32[]{:S(2)}, u32[]{:S(2)}) %collective-permute-start) | collective-permute-done | bytes 655392 | tf_op jit(solution)/shard_map/ppermute | solution.py:46
  17.5 0.8 copy-done.2
  18.3 0.0 collective-permute-start.1
  18.3 10.1 %collective-permute-done.1 = bf16[1024,320]{0,1:T(8,128)(2,1)} collective-permute-done((bf16[1024,320]{0,1:T(8,128)(2,1)S(1)}, bf16[1024,320]{0,1:T(8,128)(2,1)}, u32[]{:S(2)}, u32[]{:S(2)}) %collective-permute-start.1) | collective-permute-done | bytes 655392 | tf_op jit(solution)/shard_map/ppermute | solution.py:46
  28.4 0.0 collective-permute-start.2
  28.4 0.8 add.123
  29.2 0.8 dynamic_slice.11
  30.0 0.1 iota_compare_fusion
  30.1 8.7 %collective-permute-done.2 = bf16[1024,320]{0,1:T(8,128)(2,1)} collective-permute-done((bf16[1024,320]{0,1:T(8,128)(2,1)}, bf16[1024,320]{0,1:T(8,128)(2,1)}, u32[]{:S(2)}, u32[]{:S(2)}) %collective-permute-start.2) | collective-permute-done | bytes 655392 | tf_op jit(solution)/shard_map/ppermute | solution.py:46
  38.7 1.1 constant_dynamic-update-slice_fusion.7
  39.9 1.1 constant_dynamic-update-slice_fusion.6
  41.1 1.1 constant_dynamic-update-slice_fusion.3
  42.3 1.1 constant_dynamic-update-slice_fusion.2
  43.5 0.0 copy-start.7
  43.5 0.0 copy-start.8
  43.5 0.8 convert_reduce_fusion
  44.3 1.1 fusion.4
  45.4 4.1 %add_convert_fusion = bf16[1024,960]{0,1:T(8,128)(2,1)} fusion(f32[960]{0:T(1024)S(1)} %add.123, bf16[1280,960]{0,1:T(8,128)(2,1)S(1)} %bitcast.68, f32[1280]{0:T(1024)S(1)} %copy-done.7, f32[1280]{0:T(1024)S(1)} %copy-done.8, f32[1024]{0:T(1024)S(1)} %add_rsqrt_fusion.1, f32[1024]{0:T(1024)S(1)} %broadcast_multiply_fusion.1, ...), kind=kOutput, calls=%fused_computation.17 | convolution fusion | flops 2526412800 | bytes 7073796 | tf_op jit(solution)/shard_map/dot_general | solution.py:54
  49.6 5.8 %reshape.191 = bf16[2,512,3,4,80]{1,0,4,3,2:T(2,128)(2,1)} reshape(bf16[1024,960]{0,1:T(8,128)(2,1)} %add_convert_fusion) | data formatting | bytes 3932160 | tf_op jit(solution)/shard_map/reshape | solution.py:58
  55.3 3.4 %fusion.48 = (bf16[2,512,1,4,80]{1,0,4,3,2:T(2,128)(2,1)}, bf16[2,512,1,4,80]{1,0,4,3,2:T(2,128)(2,1)}, bf16[2,512,1,4,80]{1,0,4,3,2:T(2,128)(2,1)}) fusion(bf16[2,512,3,4,80]{1,0,4,3,2:T(2,128)(2,1)} %reshape.191), kind=kLoop, calls=%fused_computation.85 | loop fusion | bytes 3932160 | tf_op jit(solution)/shard_map/slice | solution.py:61
  58.7 7.9 %fusion.49 = (f32[2,4,512]{2,1,0:T(4,128)S(1)}, f32[2,4,512,512]{2,3,1,0:T(8,128)}) fusion(pred[2,512]{1,0:T(4,128)(4,1)S(1)} %iota_compare_fusion, bf16[2,512,1,4,80]{1,0,4,3,2:T(2,128)(2,1)} %get-tuple-element.10, bf16[2,512,1,4,80]{1,0,4,3,2:T(2,128)(2,1)} %get-tuple-element.11), kind=kOutput, calls=%fused_computation.86 | convolution fusion | flops 343933440 | bytes 9716736 | tf_op jit(solution)/shard_map/sub | solution.py:70
  66.6 4.5 %fusion.35 = bf16[2,512,4,80]{1,3,2,0:T(8,128)(2,1)S(1)} fusion(f32[2,4,512,512]{2,3,1,0:T(8,128)} %get-tuple-element.19, f32[2,4,512]{2,1,0:T(4,128)S(1)} %get-tuple-element.18, bf16[2,512,1,4,80]{1,0,4,3,2:T(2,128)(2,1)} %get-tuple-element.9), kind=kOutput, calls=%fused_computation.41 | convolution fusion | flops 340066304 | bytes 9715712 | tf_op jit(solution)/shard_map/nhqk,nkhd->nqhd/dot_general | solution.py:72
  71.1 0.0 copy-start.9
  71.1 0.7 copy.45
  71.8 0.9 copy.58
  72.7 0.0 all-gather.2.cloned.1.call-update
  72.8 0.0 copy-start.5
  72.8 0.0 copy-start.6
  72.8 0.0 all-reduce.4.cloned.1.call-start
  72.8 27.6 %all-gather.2.cloned.1.call-done = bf16[1024,1280]{0,1:T(8,128)(2,1)} async-done(((bf16[1024,320]{0,1:T(8,128)(2,1)}), bf16[1024,1280]{0,1:T(8,128)(2,1)}) %all-gather.2.cloned.1.call-update) | async-done | bytes 2621456 | tf_op jit(solution)/shard_map/all_gather | solution.py:76
  100.5 4.1 %fusion.47 = (f32[1024]{0:T(1024)S(1)}, f32[1024]{0:T(1024)S(1)}, f32[1024,320]{0,1:T(8,128)}) fusion(f32[320]{0:T(512)S(1)} %copy-done.9, bf16[1280,320]{0,1:T(8,128)(2,1)} %param.18, bf16[1024,1280]{0,1:T(8,128)(2,1)} %all-gather.2.cloned.1.call-done, bf16[1024,320]{0,1:T(8,128)(2,1)S(1)} %copy-done.1), kind=kOutput, calls=%fused_computation.84 | convolution fusion | flops 840824832 | bytes 5416192 | tf_op jit(solution)/shard_map/dot_general | solution.py:79
  104.6 6.0 %all-reduce.1 = (f32[1024]{0:T(1024)S(1)}, f32[1024]{0:T(1024)S(1)}) all-reduce(f32[1024]{0:T(1024)S(1)} %get-tuple-element.6, f32[1024]{0:T(1024)S(1)} %get-tuple-element.5), channel_id=1, replica_groups=mesh['dp'=8,'tensor'=4] {'tensor'}, use_global_device_ids=true, to_apply=%region_8.9 | all-reduce | flops 2048 | bytes 16384 | tf_op jit(solution)/shard_map/psum | solution.py:82
  110.6 2.4 add_convert_fusion.1
  113.0 1.4 copy.46
  114.4 1.6 reshape.193
  116.0 1.6 collective-permute-start.3
  117.7 14.8 %collective-permute-done.3 = bf16[256,1280]{1,0:T(8,128)(2,1)S(1)} collective-permute-done((bf16[256,1280]{1,0:T(8,128)(2,1)}, bf16[256,1280]{1,0:T(8,128)(2,1)S(1)}, u32[]{:S(2)}, u32[]{:S(2)}) %collective-permute-start.3) | collective-permute-done | bytes 655392 | tf_op jit(solution)/shard_map/ppermute | solution.py:17
  132.5 2.8 maximum_select_fusion.2
  135.2 1.5 collective-permute-start.4
  136.7 2.4 collective-permute-start.5
  139.1 53.7 %collective-permute-done.4 = bf16[512,1280]{1,0:T(8,128)(2,1)} collective-permute-done((bf16[512,1280]{1,0:T(8,128)(2,1)}, bf16[512,1280]{1,0:T(8,128)(2,1)}, u32[]{:S(2)}, u32[]{:S(2)}) %collective-permute-start.4) | collective-permute-done | bytes 1310752 | tf_op jit(solution)/shard_map/ppermute | solution.py:17
  192.9 2.8 maximum_select_fusion
  195.7 0.0 copy-start.4
  195.7 0.0 copy-start.10
  195.7 7.0 %fusion.28 = bf16[4,4,64,1024]{3,2,1,0:T(8,128)(2,1)} fusion(bf16[4,4,64,1280]{3,2,1,0:T(8,128)(2,1)S(1)} %bitcast.71, bf16[1280,512]{1,0:T(8,128)(2,1)} %bitcast.7, bf16[1280,512]{1,0:T(8,128)(2,1)} %bitcast.6, pred[]{:T(512)S(6)} %eq.34), kind=kOutput, calls=%fused_computation.34 | convolution fusion | flops 2697199616 | bytes 7340033 | tf_op jit(solution)/shard_map/dot_general | solution.py:146
  202.7 0.0 all-reduce.4.cloned.1.call-update
  202.7 0.6 dynamic-slice
  203.3 49.8 %all-reduce.4.cloned.1.call-done = bf16[4,4,64,1024]{3,2,1,0:T(8,128)(2,1)} async-done(((bf16[4,4,64,1024]{3,2,1,0:T(8,128)(2,1)}), bf16[4,4,64,1024]{3,2,1,0:T(8,128)(2,1)}) %all-reduce.4.cloned.1.call-update) | async-done | bytes 2097168
  253.1 1.8 add_convert_fusion.2
  255.0 1.5 collective-permute-start.6
  256.5 6.3 %collective-permute-done.6 = bf16[2,1,1,64,1024]{4,3,1,0,2:T(8,128)(2,1)S(1)} collective-permute-done((bf16[2,1,1,64,1024]{4,3,1,0,2:T(8,128)(2,1)S(1)}, bf16[2,1,1,64,1024]{4,3,1,0,2:T(8,128)(2,1)S(1)}, u32[]{:S(2)}, u32[]{:S(2)}) %collective-permute-start.6) | collective-permute-done | bytes 262176 | tf_op jit(solution)/shard_map/ppermute | solution.py:17
  262.8 0.1 maximum_select_fusion.3
  262.9 0.7 broadcast_select_fusion.4
  263.7 1.5 collective-permute-start.7
  265.1 0.1 fusion.40
  265.2 0.2 concatenate.80
  265.4 0.3 copy.48
  265.7 5.1 %collective-permute-done.7 = bf16[1,1,2,64,1024]{4,3,1,0,2:T(8,128)(2,1)S(1)} collective-permute-done((bf16[1,1,2,64,1024]{4,3,1,0,2:T(8,128)(2,1)}, bf16[1,1,2,64,1024]{4,3,1,0,2:T(8,128)(2,1)S(1)}, u32[]{:S(2)}, u32[]{:S(2)}) %collective-permute-start.7) | collective-permute-done | bytes 262176 | tf_op jit(solution)/shard_map/ppermute | solution.py:17
  270.8 0.2 concatenate.79
  271.0 0.3 copy.47
  271.3 1.0 fusion.39
  272.2 0.4 reshape.196
  272.6 0.9 broadcast_select_fusion
  (28 shorter events, 0.3 us)
Async XLA Ops:
  6.5 38.9 %copy-start = (bf16[1280,3,320]{0,2,1:T(8,128)(2,1)S(1)}, bf16[1280,3,320]{0,2,1:T(8,128)(2,1)}, u32[]{:S(2)}) copy-start(bf16[1280,3,320]{0,2,1:T(8,128)(2,1)} %param.16) | copy-start | bytes 7372804
  6.5 34.5 %copy-start.1 = (bf16[1024,320]{0,1:T(8,128)(2,1)S(1)}, bf16[1024,320]{0,1:T(8,128)(2,1)}, u32[]{:S(2)}) copy-start(bf16[1024,320]{0,1:T(8,128)(2,1)} %param.12) | copy-start | bytes 1966084
  6.5 93.9 %all-gather.2.cloned.1.call-start = ((), (), s32[]{:S(2)}) async-start(), calls=%async_computation | async-start | bytes 3276800 | tf_op jit(solution)/shard_map/all_gather | solution.py:76
  6.5 10.9 %collective-permute-start = (bf16[1024,320]{0,1:T(8,128)(2,1)}, bf16[1024,320]{0,1:T(8,128)(2,1)S(1)}, u32[]{:S(2)}, u32[]{:S(2)}) collective-permute-start(bf16[1024,320]{0,1:T(8,128)(2,1)} %param.12), channel_id=1, source_target_pairs={{0,1},{1,2},{2,3},{3,0},{4,5},{5,6},{6,7},{7,4},{8,9},{9,10},{10,1... | collective-permute-start | bytes 1966088 | tf_op jit(solution)/shard_map/ppermute | solution.py:46
  17.5 0.8 copy-start.2
  18.3 10.1 %collective-permute-start.1 = (bf16[1024,320]{0,1:T(8,128)(2,1)S(1)}, bf16[1024,320]{0,1:T(8,128)(2,1)}, u32[]{:S(2)}, u32[]{:S(2)}) collective-permute-start(bf16[1024,320]{0,1:T(8,128)(2,1)S(1)} %collective-permute-done), channel_id=1, source_target_pairs={{0,1},{1,2},{2,3},{3,0},{4,5},{5,6},{6,7},{7,4},{8,9},{9,10},{10,1... | collective-permute-start | bytes 1966088 | tf_op jit(solution)/shard_map/ppermute | solution.py:46
  28.4 10.3 %collective-permute-start.2 = (bf16[1024,320]{0,1:T(8,128)(2,1)}, bf16[1024,320]{0,1:T(8,128)(2,1)}, u32[]{:S(2)}, u32[]{:S(2)}) collective-permute-start(bf16[1024,320]{0,1:T(8,128)(2,1)} %collective-permute-done.1), channel_id=1, source_target_pairs={{0,1},{1,2},{2,3},{3,0},{4,5},{5,6},{6,7},{7,4},{8,9},{9,10},{10,1... | collective-permute-start | bytes 1966088 | tf_op jit(solution)/shard_map/ppermute | solution.py:46
  29.2 11.8 %copy-start.3 = (bf16[1024,320]{0,1:T(8,128)(2,1)S(1)}, bf16[1024,320]{0,1:T(8,128)(2,1)}, u32[]{:S(2)}) copy-start(bf16[1024,320]{0,1:T(8,128)(2,1)} %copy-done.2) | copy-start | bytes 1966084
  43.5 1.9 copy-start.7
  43.5 1.9 copy-start.8
  71.1 29.4 %copy-start.9 = (f32[320]{0:T(512)S(1)}, f32[320]{0:T(512)}, u32[]{:S(2)}) copy-start(f32[320]{0:T(512)} %param.19) | copy-start | bytes 3844
  72.8 37.8 %copy-start.5 = (f32[320]{0:T(512)S(1)}, f32[320]{0:T(512)}, u32[]{:S(2)}) copy-start(f32[320]{0:T(512)} %param.21) | copy-start | bytes 3844
  72.8 37.8 %copy-start.6 = (f32[320]{0:T(512)S(1)}, f32[320]{0:T(512)}, u32[]{:S(2)}) copy-start(f32[320]{0:T(512)} %param.20) | copy-start | bytes 3844
  72.8 180.3 %all-reduce.4.cloned.1.call-start = ((), (), s32[]{:S(2)}) async-start(), calls=%async_computation.1 | async-start | bytes 4194304
  116.0 16.4 %collective-permute-start.3 = (bf16[256,1280]{1,0:T(8,128)(2,1)}, bf16[256,1280]{1,0:T(8,128)(2,1)S(1)}, u32[]{:S(2)}, u32[]{:S(2)}) collective-permute-start(bf16[256,1280]{1,0:T(8,128)(2,1)} %reshape.193), channel_id=1, source_target_pairs={{0,4},{4,0},{8,12},{12,8},{16,20},{20,16},{24,28},{28,24},{1,5},{5... | collective-permute-start | bytes 1966088 | tf_op jit(solution)/shard_map/ppermute | solution.py:17
  135.2 57.6 %collective-permute-start.4 = (bf16[512,1280]{1,0:T(8,128)(2,1)}, bf16[512,1280]{1,0:T(8,128)(2,1)}, u32[]{:S(2)}, u32[]{:S(2)}) collective-permute-start(bf16[512,1280]{1,0:T(8,128)(2,1)} %maximum_select_fusion.2), channel_id=1, source_target_pairs={{0,8},{4,12},{8,0},{12,4},{16,24},{20,28},{24,16},{28,20},{1,9},{5... | collective-permute-start | bytes 3932168 | tf_op jit(solution)/shard_map/ppermute | solution.py:17
  136.7 58.9 %collective-permute-start.5 = (bf16[4,320,512]{2,1,0:T(8,128)(2,1)}, bf16[4,320,512]{2,1,0:T(8,128)(2,1)}, u32[]{:S(2)}, u32[]{:S(2)}) collective-permute-start(bf16[4,320,512]{2,1,0:T(8,128)(2,1)} %param.22), channel_id=1, source_target_pairs={{0,16},{4,20},{8,24},{12,28},{16,0},{20,4},{24,8},{28,12},{1,17},{... | collective-permute-start | bytes 3932168 | tf_op jit(solution)/shard_map/ppermute | solution.py:17
  195.7 7.0 %copy-start.4 = (f32[4096]{0:T(1024)S(1)}, f32[4096]{0:T(1024)}, u32[]{:S(2)}) copy-start(f32[4096]{0:T(1024)} %param.23) | copy-start | bytes 49156
  195.7 7.0 %copy-start.10 = (u32[32]{0:T(128)S(1)}, u32[32]{0:T(128)}, u32[]{:S(2)}) copy-start(u32[32]{0:T(128)} %constant.94) | copy-start | bytes 388
  255.0 7.9 %collective-permute-start.6 = (bf16[2,1,1,64,1024]{4,3,1,0,2:T(8,128)(2,1)S(1)}, bf16[2,1,1,64,1024]{4,3,1,0,2:T(8,128)(2,1)S(1)}, u32[]{:S(2)}, u32[]{:S(2)}) collective-permute-start(bf16[2,1,1,64,1024]{4,3,1,0,2:T(8,128)(2,1)S(1)} %get-tuple-element.14), channel_id=1, source_target_pairs={{0,4},{4,0},{8,12},{12,8},{16,20},{20,16},{24,28},{28,24},{1,5},{5... | collective-permute-start | bytes 786440 | tf_op jit(solution)/shard_map/ppermute | solution.py:17
  263.7 7.2 %collective-permute-start.7 = (bf16[1,1,2,64,1024]{4,3,1,0,2:T(8,128)(2,1)}, bf16[1,1,2,64,1024]{4,3,1,0,2:T(8,128)(2,1)S(1)}, u32[]{:S(2)}, u32[]{:S(2)}) collective-permute-start(bf16[1,1,2,64,1024]{4,3,1,0,2:T(8,128)(2,1)} %get-tuple-element.12), channel_id=1, source_target_pairs={{0,8},{4,12},{8,0},{12,4},{16,24},{20,28},{24,16},{28,20},{1,9},{5... | collective-permute-start | bytes 786440 | tf_op jit(solution)/shard_map/ppermute | solution.py:17
Sparse Core Ops, SparseCore 0:
  72.9 27.5 all-gather.1
  202.8 50.2 all-reduce.3
